TPU v7x, 32 devices: a whole 2x2x4 slice. The times are simulated.
32 devices in a mesh: grp: 2 (over y), bn: 16 (over z, x, core).
Axes of the slice: x: 2, y: 2, z: 4, core: 2. Of those that a mesh axis runs over, the one named last changes fastest.
Arguments:
- images: bfloat16 [32, 19, 19, 384], P(('grp', 'bn')), parts along dimension 0, may hold values from -56 to 56
- expand_weight: bfloat16 [384, 2304], P('bn'), may hold values from -0.3125 to 0.3125
- expand_gain: float32 [2304], replicated, may hold values from 0.5 to 2
- expand_shift: float32 [2304], replicated, may hold values from -3 to 3
- depth_weight: bfloat16 [25, 2304], replicated, may hold values from -1.25 to 1.25
- depth_gain: float32 [2304], replicated, may hold values from 0.5 to 2
- depth_shift: float32 [2304], replicated, may hold values from -3 to 3
- squeeze_weight: bfloat16 [2304, 96], replicated, may hold values from -0.125 to 0.125
- squeeze_bias: float32 [96], replicated, may hold values from -4 to 4
- excite_weight: bfloat16 [96, 2304], replicated, may hold values from -0.625 to 0.625
- excite_bias: float32 [2304], replicated, may hold values from -4 to 4
- project_weight: bfloat16 [2304, 384], P('bn'), may hold values from -0.125 to 0.125
- project_gain: float32 [384], replicated, may hold values from 0.5 to 2
- project_shift: float32 [384], replicated, may hold values from -3 to 3
- group_table: int32 [32], P('grp'), parts along dimension 0, may hold values from 0 to 1, as said below
Outputs:
- block_output: bfloat16 [32, 19, 19, 384], P(('grp', 'bn')), parts along dimension 0
There are 2 independent parts, one for each index of `grp`. A program takes and returns all parts, laid end to end along the dimension named above; an argument that names none is the same for every part. Nothing has to cross between parts.
Inputs may be any that keep to these rules, and one draw needn't show every extreme that they name: `group_table`: each of the 2 statistics groups holds at least 4 images, placed anywhere among the images.
All inputs are finite; a program needn't handle non-finite values.
Results may differ from a plain program's by a relative error of at most 0.0065.
Values may be sent and summed in bfloat16 or wider, within the bound.
A program may use at most 64 MiB of HBM per device.

v0:
```python
import jax
import jax.numpy as jnp
from jax import lax
from jax.sharding import PartitionSpec as P

KERNEL = 5
STAT_GROUPS = 2


epsilon = 0.001


def normalize(values, centre, inverse, gain, shift):
    return (values.astype(jnp.float32) - centre) * inverse * gain + shift


def depthwise(widened, depth_weight, height, breadth):
    spatial = widened.reshape(height, breadth, widened.shape[-1])
    margin = KERNEL // 2
    padded = jnp.pad(spatial, ((margin, margin), (margin, margin), (0, 0)))
    accumulated = jnp.zeros(spatial.shape, jnp.float32)
    for row_shift in range(KERNEL):
        for col_shift in range(KERNEL):
            window = padded[row_shift : row_shift + height, col_shift : col_shift + breadth]
            accumulated = accumulated + window.astype(jnp.float32) * depth_weight[
                row_shift * KERNEL + col_shift
            ].astype(jnp.float32)
    return accumulated.reshape(height * breadth, spatial.shape[-1]).astype(jnp.bfloat16)


def group_moments(values, selector, population):
    totals = jnp.sum(values, axis=0, dtype=jnp.float32)
    squares = jnp.sum(jnp.square(values.astype(jnp.float32)), axis=0)
    weighted = selector[:, None, None] * jnp.stack([totals, squares])[None]
    summed = lax.psum(weighted, "bn")
    picked = jnp.sum(selector[:, None, None] * summed, axis=0)
    centre = picked[0] / population
    spread = picked[1] / population - centre * centre
    return (centre, lax.rsqrt(spread + epsilon))


def on_device(
    images,
    expand_weight,
    expand_gain,
    expand_shift,
    depth_weight,
    depth_gain,
    depth_shift,
    squeeze_weight,
    squeeze_bias,
    excite_weight,
    excite_bias,
    project_weight,
    project_gain,
    project_shift,
    group_table,
):
    height, breadth, channels = (images.shape[1], images.shape[2], images.shape[3])
    pixels = height * breadth
    flattened = images.reshape(pixels, channels)
    device_rank = lax.axis_index("bn")
    ranks_all = jnp.arange(group_table.shape[0], dtype=jnp.int32)
    my_group = jnp.sum(jnp.where(ranks_all == device_rank, group_table, 0))
    members = jnp.sum((group_table == my_group).astype(jnp.float32))
    population = members * pixels
    selector = (jnp.arange(STAT_GROUPS, dtype=jnp.int32) == my_group).astype(jnp.float32)
    inputs = flattened
    expanded = jnp.dot(
        inputs,
        lax.all_gather(expand_weight, "bn", axis=0, tiled=True),
        preferred_element_type=jnp.float32,
    ).astype(jnp.bfloat16)
    centre, inverse = group_moments(expanded, selector, population)
    widened = jax.nn.silu(normalize(expanded, centre, inverse, expand_gain, expand_shift)).astype(
        jnp.bfloat16
    )
    filtered = depthwise(widened, depth_weight, height, breadth)
    centre, inverse = group_moments(filtered, selector, population)
    activated = jax.nn.silu(normalize(filtered, centre, inverse, depth_gain, depth_shift)).astype(
        jnp.bfloat16
    )
    pooled = (jnp.sum(activated, axis=0, dtype=jnp.float32) / pixels).astype(jnp.bfloat16)[None, :]
    squeezed = jax.nn.silu(
        jnp.dot(pooled, squeeze_weight, preferred_element_type=jnp.float32) + squeeze_bias
    ).astype(jnp.bfloat16)
    excitation = jax.nn.sigmoid(
        jnp.dot(squeezed, excite_weight, preferred_element_type=jnp.float32) + excite_bias
    )
    gated_input = (activated * excitation).astype(jnp.bfloat16)
    inputs = gated_input
    projected = jnp.dot(
        inputs,
        lax.all_gather(project_weight, "bn", axis=0, tiled=True),
        preferred_element_type=jnp.float32,
    ).astype(jnp.bfloat16)
    centre, inverse = group_moments(projected, selector, population)
    output = flattened.astype(jnp.float32) + normalize(
        projected, centre, inverse, project_gain, project_shift
    )
    return output.astype(jnp.bfloat16).reshape(images.shape)


def solution(mesh):
    return jax.shard_map(
        on_device,
        mesh=mesh,
        in_specs=(
            P(("grp", "bn"), None, None, None),
            P("bn", None),
            P(),
            P(),
            P(),
            P(),
            P(),
            P(),
            P(),
            P(),
            P(),
            P("bn", None),
            P(),
            P(),
            P("grp"),
        ),
        out_specs=P(("grp", "bn"), None, None, None),
        check_vma=False,
    )
```

profile of v0, /device:TPU:0, one launch (start us, length us, event | category | flops | bytes accessed | tf_op | source)
XLA Modules:
  0.0 257.8 jit_solution(15007953222312947867)
XLA Ops:
  6.5 0.7 all-gather.3.cloned.1.call-update
  7.3 0.7 all-gather.5.cloned.1.call-update
  8.0 1.3 fusion.15
  9.3 0.6 compare_convert_fusion.1
  10.0 1.9 fusion.16
  11.9 1.9 convert_reduce_fusion.27
  13.7 1.1 convert_reduce_fusion.26
  14.9 1.1 reshape.239
  16.6 36.0 %all-gather.3.cloned.1.call-done = bf16[384,2304]{1,0:T(8,128)(2,1)} async-done(((bf16[24,2304]{1,0:T(8,128)(2,1)}), bf16[384,2304]{1,0:T(8,128)(2,1)}) %all-gather.3.cloned.1.call-update) | async-done | bytes 1769488 | tf_op jit(solution)/shard_map/all_gather | solution.py:71
  52.5 3.7 %convert_reduce_fusion = (f32[2304]{0:T(1024)S(1)}, f32[2304]{0:T(1024)S(1)}, bf16[361,2304]{1,0:T(8,128)(2,1)}) fusion(bf16[361,384]{1,0:T(8,128)(2,1)S(1)} %reshape.239, bf16[384,2304]{1,0:T(8,128)(2,1)} %all-gather.3.cloned.1.call-done), kind=kOutput, calls=%fused_computation.2 | convolution fusion | flops 642933504 | bytes 3728640 | tf_op jit(solution)/shard_map/dot_general | solution.py:69
  56.4 59.8 %psum.21 = f32[2,2,2304]{2,1,0:T(2,128)S(1)} all-reduce(f32[2,2,2304]{2,1,0:T(2,128)S(1)} %broadcast_multiply_fusion.1), channel_id=1, replica_groups=mesh['grp'=2,'bn'=16] {'bn'}, use_global_device_ids=true, to_apply=%region_3.4 | all-reduce | flops 9216 | bytes 73728 | tf_op jit(solution)/shard_map/psum | solution.py:35
  116.2 0.1 multiply_reduce_fusion.3
  116.4 2.6 %fusion.9 = bf16[361,2304]{1,0:T(8,128)(2,1)S(1)} fusion(bf16[361,2304]{1,0:T(8,128)(2,1)} %get-tuple-element.43, f32[2304]{0:T(1024)S(1)} %copy-done.2, f32[2304]{0:T(1024)S(1)} %copy-done.3, f32[2304]{0:T(1024)S(1)} %get-tuple-element.39, f32[2304]{0:T(1024)S(1)} %get-tuple-element.38), kind=kLoop, calls=%fused_computation.17 | loop fusion | flops 8317440 | bytes 3363840 | tf_op jit(solution)/shard_map/convert_element_type | solution.py:75
  119.0 2.0 reshape.240
  121.0 32.3 %convert_reduce_fusion.2 = (f32[2304]{0:T(1024)S(1)}, f32[2304]{0:T(1024)S(1)}, bf16[19,19,2304]{2,1,0:T(8,128)(2,1)S(1)}) fusion(f32[2304]{0:T(1024)S(1)} %get-tuple-element.34, f32[2304]{0:T(1024)S(1)} %get-tuple-element.35, f32[2304]{0:T(1024)S(1)} %get-tuple-element.12, f32[2304]{0:T(1024)S(1)} %get-tuple-element.13, f32[2304]{0:T(1024)S(1)} %get-tuple-element.14, ...), kind=kLoop, calls=%fused_computation.20 | loop fusion | flops 65703168 | bytes 3575808 | tf_op jit(solution)/shard_map/reduce_sum | solution.py:32
  153.4 2.2 reshape.267
  155.7 57.9 %psum.22 = f32[2,2,2304]{2,1,0:T(2,128)S(1)} all-reduce(f32[2,2,2304]{2,1,0:T(2,128)S(1)} %broadcast_multiply_fusion), channel_id=1, replica_groups=mesh['grp'=2,'bn'=16] {'bn'}, use_global_device_ids=true, to_apply=%region_8.9 | all-reduce | flops 9216 | bytes 73728 | tf_op jit(solution)/shard_map/psum | solution.py:35
  213.6 0.1 multiply_reduce_fusion.2
  213.8 1.6 convert_reduce_fusion.1
  215.4 0.4 convolution_reduce_fusion
  215.9 3.9 %fusion.24 = (f32[384]{0:T(512)S(1)}, f32[384]{0:T(512)S(1)}, f32[361,384]{1,0:T(8,128)S(1)}) fusion(bf16[2304,384]{1,0:T(8,128)(2,1)} %all-gather.5.cloned.1.call-done, f32[2304]{0:T(1024)S(1)} %add_divide_fusion, f32[2304]{0:T(1024)S(1)} %copy-done.4, f32[2304]{0:T(1024)S(1)} %copy-done.5, f32[2304]{0:T(1024)S(1)} %get-tuple-element.37, ...), kind=kOutput, calls=%fused_computation.106 | convolution fusion | flops 649452672 | bytes 5700096 | tf_op jit(solution)/shard_map/dot_general | solution.py:92
  219.9 30.0 %psum.23 = f32[2,2,384]{2,1,0:T(2,128)S(1)} all-reduce(f32[2,2,384]{2,1,0:T(2,128)S(1)} %broadcast_multiply_fusion.2), channel_id=1, replica_groups=mesh['grp'=2,'bn'=16] {'bn'}, use_global_device_ids=true, to_apply=%region_13.14 | all-reduce | flops 1536 | bytes 12288 | tf_op jit(solution)/shard_map/psum | solution.py:35
  250.0 0.1 add_convert_fusion.1
  250.2 0.8 reshape.241
  (42 shorter events, 0.7 us)
Async XLA Ops:
  6.5 208.8 %copy-start = (bf16[96,2304]{1,0:T(8,128)(2,1)S(1)}, bf16[96,2304]{1,0:T(8,128)(2,1)}, u32[]{:S(2)}) copy-start(bf16[96,2304]{1,0:T(8,128)(2,1)} %param.24) | copy-start | bytes 1327108
  6.5 46.0 %all-gather.3.cloned.1.call-start = ((), (), s32[]{:S(2)}) async-start(), calls=%async_computation | async-start | bytes 1880064 | tf_op jit(solution)/shard_map/all_gather | solution.py:71
  7.3 208.6 %all-gather.5.cloned.1.call-start = ((), (), s32[]{:S(2)}) async-start(), calls=%async_computation.1 | async-start | bytes 1880064 | tf_op jit(solution)/shard_map/all_gather | solution.py:94
  16.5 99.8 %copy-start.2 = (f32[2304]{0:T(1024)S(1)}, f32[2304]{0:T(1024)}, u32[]{:S(2)}) copy-start(f32[2304]{0:T(1024)} %param.18) | copy-start | bytes 27652
  16.5 99.8 %copy-start.3 = (f32[2304]{0:T(1024)S(1)}, f32[2304]{0:T(1024)}, u32[]{:S(2)}) copy-start(f32[2304]{0:T(1024)} %param.17) | copy-start | bytes 27652
  153.3 60.4 %copy-start.4 = (f32[2304]{0:T(1024)S(1)}, f32[2304]{0:T(1024)}, u32[]{:S(2)}) copy-start(f32[2304]{0:T(1024)} %param.21) | copy-start | bytes 27652
  153.3 60.4 %copy-start.5 = (f32[2304]{0:T(1024)S(1)}, f32[2304]{0:T(1024)}, u32[]{:S(2)}) copy-start(f32[2304]{0:T(1024)} %param.20) | copy-start | bytes 27652
  153.3 62.0 %copy-start.1 = (bf16[2304,96]{0,1:T(8,128)(2,1)S(1)}, bf16[2304,96]{0,1:T(8,128)(2,1)}, u32[]{:S(2)}) copy-start(bf16[2304,96]{0,1:T(8,128)(2,1)} %param.22) | copy-start | bytes 1327108
  153.3 62.0 %copy-start.9 = (f32[96]{0:T(128)S(1)}, f32[96]{0:T(128)}, u32[]{:S(2)}) copy-start(f32[96]{0:T(128)} %param.23) | copy-start | bytes 1156
  153.4 62.5 %copy-start.6 = (f32[2304]{0:T(1024)S(1)}, f32[2304]{0:T(1024)}, u32[]{:S(2)}) copy-start(f32[2304]{0:T(1024)} %param.25) | copy-start | bytes 27652
  215.8 34.2 %copy-start.7 = (f32[384]{0:T(512)S(1)}, f32[384]{0:T(512)}, u32[]{:S(2)}) copy-start(f32[384]{0:T(512)} %param.28) | copy-start | bytes 4612
  215.8 34.2 %copy-start.8 = (f32[384]{0:T(512)S(1)}, f32[384]{0:T(512)}, u32[]{:S(2)}) copy-start(f32[384]{0:T(512)} %param.27) | copy-start | bytes 4612
Sparse Core Ops, SparseCore 0:
  9.5 42.9 all-gather.2
  54.7 39.2 all-gather.4
where the time goes:
time: 258 us
  blocking collectives  148 us (57%)
  other arithmetic  44.2 us (17%)
  waiting for transfers between devices  37.4 us (14%)
  between operations  14.3 us (6%)
  matrix products  8.06 us (3%)
  local copies, waits for them, and re-layouts  6.24 us (2%)
    psum x3, blocking collectives, group_moments(): summed = lax.psum(weighted, 'bn')  148 us
    all_gather x1, waiting for transfers between devices, on_device(): lax.all_gather(expand_weight, 'bn', axis=0, tiled=True)  36 us
    reduce_sum x1, other arithmetic, group_moments(): totals = jnp.sum(values, axis=0, dtype=jnp.float32)  32.3 us
  transfers between devices with their start and end apart: 2, of which 1 were waited for; matrix products, arithmetic and copies ran while one was open for 21% of the time, Pallas kernels for 0%

commit v1 on v0

v1 whole, which is shorter than its diff:
```python
import functools

import jax
import jax.numpy as jnp
from jax import lax
from jax.experimental import pallas as pl
from jax.experimental.pallas import tpu as pltpu
from jax.sharding import PartitionSpec as P

KERNEL = 5
LANES = 128
MARGIN = KERNEL // 2
epsilon = 0.001
MESH = pl.DeviceIdType.MESH


def silu(v):
    h = 0.5 * v
    return h + h * jnp.tanh(h)


def gather_steps(n, buf, send_sem, recv_sem, rows):
    outer = n // 4
    me = lax.axis_index("bn")
    a, b, c = me // 4, (me // 2) % 2, me % 2

    def index(i, j, k):
        return (i % outer) * 4 + j * 2 + k

    sends = []

    def copy(slot, target, number):
        return pltpu.make_async_remote_copy(
            src_ref=buf.at[slot, pl.ds(0, rows)],
            dst_ref=buf.at[slot, pl.ds(0, rows)],
            send_sem=send_sem.at[number],
            recv_sem=recv_sem.at[slot],
            device_id={"bn": target},
            device_id_type=MESH,
        )

    def send(slot, target):
        move = copy(slot, target, len(sends))
        move.start()
        sends.append(move)

    def await_slot(slot):
        copy(slot, me, 0).wait_recv()

    across, partner = index(a, 1 - b, c), index(a, b, 1 - c)

    def first():
        for d in range(1, outer):
            send(me, index(a + d, b, c))
        send(me, across)
        send(me, partner)

    def second():
        for d in range(1, outer):
            slot = index(a + outer - d, b, c)
            await_slot(slot)
            send(slot, across)
            send(slot, partner)
        await_slot(across)
        send(across, partner)

    def third():
        for d in range(1, outer):
            slot = index(a + outer - d, 1 - b, c)
            await_slot(slot)
            send(slot, partner)
        for i in range(outer):
            for j in range(2):
                await_slot(index(i, j, 1 - c))

    def finish():
        for move in sends:
            move.wait_send()

    return first, second, third, finish


def kernel(
    n, inside, height, breadth, pitch, groups,
    sel_ref, x_ref, w1_ref, g1_ref, s1_ref, dw_ref, g2_ref, s2_ref,
    sqw_ref, sqb_ref, exw_ref, exb_ref, w2_ref, g3_ref, s3_ref,
    out_ref,
    xp, w1, w2, expanded, filtered, wide, narrow, coef, pooled, proj,
    stats, last, w1_send, w1_recv, w2_send, w2_recv, st_send, st_recv,
):
    me = lax.axis_index("bn")
    rows = x_ref.shape[0]
    channels = x_ref.shape[1]
    exp = expanded.shape[1]
    width = exp // groups
    pixels = float(height * breadth)

    def mask_of(lanes):
        column = lax.broadcasted_iota(jnp.int32, (height, pitch, lanes), 1)
        return (column < breadth).reshape(rows, lanes)

    def masked(v):
        lanes = v.shape[1]
        column = lax.broadcasted_iota(jnp.int32, (height, pitch, lanes), 1)
        kept = jnp.where(column < breadth, v.reshape(height, pitch, lanes), 0.0)
        return kept.reshape(rows, lanes)

    def moments(v):
        centre = jnp.sum(v, axis=0, keepdims=True) / pixels
        d = masked(v - centre)
        return jnp.concatenate(
            [centre, jnp.sum(d * d, axis=0, keepdims=True) / pixels], axis=0
        )

    def exchange(e, buf):
        def move(j):
            target = lax.rem(me + j, n)
            return pltpu.make_async_remote_copy(
                src_ref=buf.at[me],
                dst_ref=buf.at[me],
                send_sem=st_send.at[e, j],
                recv_sem=st_recv.at[e, j],
                device_id={"bn": target},
                device_id_type=MESH,
            )

        def start():
            @pl.loop(1, n)
            def _(j):
                move(j).start()

        def wait():
            @pl.loop(1, n)
            def _(j):
                source = lax.rem(me + n - j, n)
                pltpu.make_async_remote_copy(
                    src_ref=buf.at[source],
                    dst_ref=buf.at[source],
                    send_sem=st_send.at[e, j],
                    recv_sem=st_recv.at[e, j],
                    device_id={"bn": me},
                    device_id_type=MESH,
                ).wait_recv()

        def finish():
            @pl.loop(1, n)
            def _(j):
                move(j).wait_send()

        return start, wait, finish

    def combine(buf, gain, shift):
        centre = jnp.zeros(gain.shape, jnp.float32)
        for k in range(n):
            centre = centre + sel_ref[k] * buf[k, 0:1, :]
        spread = jnp.zeros(gain.shape, jnp.float32)
        for k in range(n):
            d = buf[k, 0:1, :] - centre
            spread = spread + sel_ref[k] * (buf[k, 1:2, :] + d * d)
        scale = lax.rsqrt(spread + epsilon) * gain
        return scale, shift - centre * scale

    r1, r2 = w1_ref.shape[0], w2_ref.shape[0]
    if inside:
        slab = w1.shape[1]
        if slab != r1:
            w1[...] = jnp.zeros_like(w1)
        w1[me, 0:r1, :] = w1_ref[...]
        w2[me] = w2_ref[...]
        g1 = gather_steps(n, w1, w1_send, w1_recv, r1)
        g2 = gather_steps(n, w2, w2_send, w2_recv, r2)

    barrier = pltpu.get_barrier_semaphore()

    @pl.loop(1, n)
    def _(j):
        pl.semaphore_signal(
            barrier, inc=1, device_id={"bn": lax.rem(me + j, n)}, device_id_type=MESH
        )

    pl.semaphore_wait(barrier, n - 1)

    if inside:
        g1[0]()
        k = lax.broadcasted_iota(jnp.int32, (channels, n * slab), 0)
        j = lax.broadcasted_iota(jnp.int32, (channels, n * slab), 1)
        bits = slab.bit_length() - 1
        t = jnp.bitwise_and(j, slab - 1)
        target = jnp.right_shift(j, bits) * r1 + t
        spreader = jnp.where((k == target) & (t < r1), 1.0, 0.0).astype(jnp.bfloat16)
        xp[...] = jnp.dot(
            x_ref[...], spreader, preferred_element_type=jnp.float32
        ).astype(jnp.bfloat16)
    wide[...] = jnp.zeros_like(wide)
    if inside:
        g1[1]()
        g1[2]()

    step = 256
    steps = width // step
    first_ex = [exchange(g, stats.at[0, g]) for g in range(groups)]
    second_ex = [exchange(groups + g, stats.at[1, g]) for g in range(groups)]
    third_ex = exchange(2 * groups, last)

    for g in range(groups):
        @pl.loop(0, steps)
        def _(i):
            inner = pl.ds(pl.multiple_of(i * step, step), step)
            cols = pl.ds(pl.multiple_of(g * width + i * step, step), step)
            if inside:
                weights = w1[:, :, cols].reshape(n * slab, step)
                v = jnp.dot(xp[...], weights, preferred_element_type=jnp.float32)
            else:
                v = jnp.dot(x_ref[...], w1_ref[:, cols], preferred_element_type=jnp.float32)
            v = v.astype(jnp.bfloat16)
            expanded[:, cols] = v
            stats[0, g, me, :, inner] = moments(v.astype(jnp.float32))

        first_ex[g][0]()

    if inside:
        g2[0]()

    top = MARGIN * pitch
    small = width // LANES
    for g in range(groups):
        first_ex[g][1]()
        base = pl.ds(g * width, width)
        scale, offset = combine(stats.at[0, g], g1_ref[:, base], s1_ref[:, base])
        coef[0:1, base] = scale
        coef[1:2, base] = offset

        @pl.loop(0, small)
        def _(i):
            inner = pl.ds(pl.multiple_of(i * LANES, LANES), LANES)
            cols = pl.ds(pl.multiple_of(g * width + i * LANES, LANES), LANES)
            v = expanded[:, cols].astype(jnp.float32) * coef[0:1, cols] + coef[1:2, cols]
            wide[pl.ds(top, rows), :] = masked(silu(v))

            def row(y, carry):
                window = [
                    wide[pl.ds(pl.multiple_of((y + r) * pitch, 8), pitch), :]
                    for r in range(KERNEL)
                ]
                total = None
                for s in range(KERNEL):
                    part = None
                    for r in range(KERNEL):
                        tap = r * KERNEL + s
                        term = window[r] * dw_ref[tap : tap + 1, cols]
                        part = term if part is None else part + term
                    turn = (MARGIN - s) % pitch
                    if turn:
                        part = pltpu.roll(part, turn, 0)
                    total = part if total is None else total + part
                narrow[pl.ds(pl.multiple_of(y * pitch, 8), pitch), :] = total
                return carry

            lax.fori_loop(0, height, row, 0, unroll=True)
            f = masked(narrow[...]).astype(jnp.bfloat16)
            filtered[:, cols] = f
            stats[1, g, me, :, inner] = moments(f.astype(jnp.float32))

        second_ex[g][0]()
        if inside and g == groups - 1:
            g2[1]()

    for g in range(groups):
        second_ex[g][1]()
        base = pl.ds(g * width, width)
        scale, offset = combine(stats.at[1, g], g2_ref[:, base], s2_ref[:, base])
        coef[0:1, base] = scale
        coef[1:2, base] = offset

        @pl.loop(0, small)
        def _(i):
            cols = pl.ds(pl.multiple_of(g * width + i * LANES, LANES), LANES)
            v = filtered[:, cols].astype(jnp.float32) * coef[0:1, cols] + coef[1:2, cols]
            v = masked(silu(v))
            filtered[:, cols] = v.astype(jnp.bfloat16)
            pooled[:, cols] = jnp.broadcast_to(
                jnp.sum(v, axis=0, keepdims=True) / pixels, (8, LANES)
            )

    squeezed = silu(
        jnp.dot(
            pooled[...].astype(jnp.bfloat16), sqw_ref[...], preferred_element_type=jnp.float32
        )
        + sqb_ref[...]
    ).astype(jnp.bfloat16)
    gate = (
        jnp.dot(squeezed, exw_ref[...], preferred_element_type=jnp.float32) + exb_ref[...]
    )
    pooled[...] = 0.5 + 0.5 * jnp.tanh(0.5 * gate)

    @pl.loop(0, exp // LANES)
    def _(i):
        cols = pl.ds(pl.multiple_of(i * LANES, LANES), LANES)
        filtered[:, cols] = (
            filtered[:, cols].astype(jnp.float32) * pooled[0:1, cols]
        ).astype(jnp.bfloat16)

    if inside:
        g2[2]()
        weights = w2[...].reshape(n * r2, channels)
    else:
        weights = w2_ref[...]
    proj[...] = jnp.dot(filtered[...], weights, preferred_element_type=jnp.float32)
    last[me] = moments(proj[...])
    third_ex[0]()
    third_ex[1]()
    scale, offset = combine(last, g3_ref[...], s3_ref[...])
    out_ref[...] = (
        x_ref[...].astype(jnp.float32) + (proj[...] * scale + offset)
    ).astype(jnp.bfloat16)

    for e in first_ex + second_ex + [third_ex]:
        e[2]()
    if inside:
        g1[3]()
        g2[3]()


def on_device(
    n, images, expand_weight, expand_gain, expand_shift, depth_weight, depth_gain,
    depth_shift, squeeze_weight, squeeze_bias, excite_weight, excite_bias,
    project_weight, project_gain, project_shift, group_table,
):
    height, breadth, channels = images.shape[1:]
    exp = expand_weight.shape[1]
    pitch = -(-(breadth + MARGIN) // 8) * 8
    rows = height * pitch
    r1, r2 = expand_weight.shape[0], project_weight.shape[0]
    inside = n % 4 == 0 and r1 % 8 == 0 and r2 % 16 == 0
    slab = 16
    while slab < r1:
        slab *= 2
    groups = 3 if exp % (3 * 256) == 0 else 1
    if not inside:
        expand_weight = lax.all_gather(expand_weight, "bn", axis=0, tiled=True)
        project_weight = lax.all_gather(project_weight, "bn", axis=0, tiled=True)
    me = lax.axis_index("bn")
    ranks = jnp.arange(n, dtype=jnp.int32)
    mine = jnp.sum(jnp.where(ranks == me, group_table, 0))
    member = (group_table == mine).astype(jnp.float32)
    sel = member / jnp.sum(member)
    x = jnp.pad(images[0], ((0, 0), (0, pitch - breadth), (0, 0))).reshape(rows, channels)
    f32, bf16 = jnp.float32, jnp.bfloat16
    small = (1, 16, LANES)
    vmem = pl.BlockSpec(memory_space=pltpu.VMEM)
    exchanges = 2 * groups + 1
    out = pl.pallas_call(
        functools.partial(kernel, n, inside, height, breadth, pitch, groups),
        out_shape=jax.ShapeDtypeStruct((rows, channels), bf16),
        in_specs=[pl.BlockSpec(memory_space=pltpu.SMEM)] + [vmem] * 14,
        out_specs=vmem,
        scratch_shapes=[
            pltpu.VMEM((rows, n * slab) if inside else (16, LANES), bf16),
            pltpu.VMEM((n, slab, exp) if inside else small, bf16),
            pltpu.VMEM((n, r2, channels) if inside else small, bf16),
            pltpu.VMEM((rows, exp), bf16),
            pltpu.VMEM((rows, exp), bf16),
            pltpu.VMEM((rows + 2 * MARGIN * pitch, LANES), f32),
            pltpu.VMEM((rows, LANES), f32),
            pltpu.VMEM((2, exp), f32),
            pltpu.VMEM((8, exp), f32),
            pltpu.VMEM((rows, channels), f32),
            pltpu.VMEM((2, groups, n, 2, exp // groups), f32),
            pltpu.VMEM((n, 2, channels), f32),
            pltpu.SemaphoreType.DMA((n,)),
            pltpu.SemaphoreType.DMA((n,)),
            pltpu.SemaphoreType.DMA((n,)),
            pltpu.SemaphoreType.DMA((n,)),
            pltpu.SemaphoreType.DMA((exchanges, n)),
            pltpu.SemaphoreType.DMA((exchanges, n)),
        ],
        compiler_params=pltpu.CompilerParams(
            collective_id=0, has_side_effects=True, vmem_limit_bytes=60 * 1024 * 1024
        ),
    )(
        sel, x, expand_weight, expand_gain[None], expand_shift[None],
        depth_weight.astype(f32), depth_gain[None], depth_shift[None],
        squeeze_weight, squeeze_bias[None], excite_weight, excite_bias[None],
        project_weight, project_gain[None], project_shift[None],
    )
    return out.reshape(height, pitch, channels)[None, :, :breadth]


def solution(mesh):
    n = mesh.shape["bn"]
    return jax.shard_map(
        functools.partial(on_device, n),
        mesh=mesh,
        in_specs=(
            P(("grp", "bn"), None, None, None),
            P("bn", None),
            P(), P(), P(), P(), P(), P(), P(), P(), P(),
            P("bn", None),
            P(), P(),
            P("grp"),
        ),
        out_specs=P(("grp", "bn"), None, None, None),
        check_vma=False,
    )
```

time: 258 us -> 85 us (0.33)
  blocking collectives: 148 us -> 0 us
  Pallas kernels: 0 us -> 64.7 us
  other arithmetic: 44.2 us -> 6.79 us
  waiting for transfers between devices: 37.4 us -> 0 us
  between operations: 14.3 us -> 0.75 us
  matrix products: 8.06 us -> 0 us
  local copies, waits for them, and re-layouts: 6.24 us -> 12.3 us
    psum x3 -> x0, blocking collectives: 148 us -> none  [group_moments(): summed = lax.psum(weighted, 'bn')]
    pallas_call x0 -> x1, Pallas kernels: none -> 64.7 us  [on_device(): pl.pallas_call(functools.partial(kernel, n, inside, height, breadth, pitc...]
    all_gather x2 -> x0, waiting for transfers between devices: 36 us -> none  [the longest x1 36 us: on_device(): lax.all_gather(expand_weight, 'bn', axis=0, tiled=True)]
    reduce_sum x7 -> x2, other arithmetic: 37.3 us -> 3.33 us  [the longest x1 1.98 us: on_device(): sel = member / jnp.sum(member)]
    broadcast_in_dim x0 -> x8, local copies, waits for them, and re-layouts: none -> 10.1 us  [the longest x1 1.75 us: on_device(): return out.reshape(height, pitch, channels)[None, :, :breadth]]
    dot_general x3 -> x0, matrix products: 8.06 us -> none  [the longest x1 3.9 us: on_device(): jnp.dot(inputs, lax.all_gather(project_weight, 'bn', axis=0, tiled=True),...]
    convert_element_type x6 -> x1, other arithmetic: 6.41 us -> 1.64 us  [on_device(): depth_weight.astype(f32)]
    reshape x3 -> x0, local copies, waits for them, and re-layouts: 3.92 us -> none  [the longest x1 2.01 us: depthwise(): spatial = widened.reshape(height, breadth, widened.shape[-1])]
  transfers between devices with their start and end apart: 2 -> 0, of which waited for: 1 -> 0; matrix products, arithmetic and copies ran while one was open for 21% -> 0% of each run, Pallas kernels for 0% -> 0%
where the time goes in v1:
time: 85 us; the launch traced here: 84.5 us
  Pallas kernels  64.7 us (76%)
  local copies, waits for them, and re-layouts  12.3 us (14%)
  other arithmetic  6.79 us (8%)
    pallas_call x1, Pallas kernels, on_device(): pl.pallas_call(functools.partial(kernel, n, inside, height, breadth, pitc...  64.7 us
    reduce_sum x1, other arithmetic, on_device(): sel = member / jnp.sum(member)  1.98 us
    div x1, other arithmetic, on_device(): sel = member / jnp.sum(member)  1.82 us
    broadcast_in_dim x1, local copies, waits for them, and re-layouts, on_device(): return out.reshape(height, pitch, channels)[None, :, :breadth]  1.75 us

profile of v1, /device:TPU:0, one launch (start us, length us, event | category | flops | bytes accessed | tf_op | source)
XLA Modules:
  0.0 84.5 jit_solution(586341465433110678)
XLA Ops:
  0.0 0.0 copy-start.2
  0.0 0.0 copy-start.1
  0.0 1.3 %fusion.1 = s32[]{:T(128)} fusion(s32[16]{0:T(128)} %param.29, s32[]{:T(128)S(6)} %axis_index.12), kind=kLoop, calls=%fused_computation.5 | loop fusion | flops 47 | bytes 72 | tf_op jit(solution)/shard_map/reduce_sum | solution.py:344
  1.3 2.0 %fusion = f32[]{:T(128)} fusion(s32[16]{0:T(128)} %param.29, s32[]{:T(128)} %fusion.1), kind=kLoop, calls=%fused_computation.4 | loop fusion | flops 47 | bytes 72 | tf_op jit(solution)/shard_map/reduce_sum | solution.py:346
  4.1 1.8 %compare_select_fusion.1.sel_ref = f32[16]{0:T(128)} fusion(s32[16]{0:T(128)} %param.29, f32[]{:T(128)S(6)} %divide.3, s32[]{:T(128)} %fusion.1), kind=kLoop, calls=%fused_computation.2 | loop fusion | flops 32 | bytes 136 | tf_op jit(solution)/shard_map/div | solution.py:346
  5.9 1.2 %broadcast_in_dim.38.g3_ref = f32[1,384]{1,0:T(1,128)} reshape(f32[384]{0:T(512)} %param.27) | data formatting | bytes 3072 | tf_op jit(solution)/shard_map/broadcast_in_dim | solution.py:384
  7.1 1.3 %broadcast_in_dim.39.s3_ref = f32[1,384]{1,0:T(1,128)} reshape(f32[384]{0:T(512)} %param.28) | data formatting | bytes 3072 | tf_op jit(solution)/shard_map/broadcast_in_dim | solution.py:384
  8.4 0.0 copy-done.2
  8.4 0.6 broadcast_in_dim.32.g1_ref
  9.0 1.3 %broadcast_in_dim.33.s1_ref = f32[1,2304]{1,0:T(1,128)} reshape(f32[2304]{0:T(1024)} %param.18) | data formatting | bytes 18432 | tf_op jit(solution)/shard_map/broadcast_in_dim | solution.py:381
  10.3 1.3 %broadcast_in_dim.34.g2_ref = f32[1,2304]{1,0:T(1,128)} reshape(f32[2304]{0:T(1024)} %param.20) | data formatting | bytes 18432 | tf_op jit(solution)/shard_map/broadcast_in_dim | solution.py:382
  11.6 1.3 %broadcast_in_dim.35.s2_ref = f32[1,2304]{1,0:T(1,128)} reshape(f32[2304]{0:T(1024)} %param.21) | data formatting | bytes 18432 | tf_op jit(solution)/shard_map/broadcast_in_dim | solution.py:382
  12.9 1.3 %broadcast_in_dim.37.exb_ref = f32[1,2304]{1,0:T(1,128)} reshape(f32[2304]{0:T(1024)} %param.25) | data formatting | bytes 18432 | tf_op jit(solution)/shard_map/broadcast_in_dim | solution.py:383
  14.2 1.6 %convert_element_type.9.dw_ref = f32[25,2304]{1,0:T(8,128)} convert(bf16[25,2304]{1,0:T(8,128)(2,1)} %param.19) | non-fusion elementwise | flops 57600 | bytes 345600 | tf_op jit(solution)/shard_map/convert_element_type | solution.py:382
  15.9 0.0 copy-done.1
  15.9 0.0 copy-start
  15.9 0.8 pad.4
  16.6 0.4 copy-done
  17.0 1.1 %copy.16.sqw_ref = bf16[2304,96]{1,0:T(8,128)(2,1)} copy(bf16[2304,96]{0,1:T(8,128)(2,1)S(1)} %copy-done) | data formatting | bytes 884736 | tf_op args[7]
  18.1 64.7 %shard_map.145 = bf16[456,384]{1,0:T(8,128)(2,1)} custom-call(f32[16]{0:T(128)} %compare_select_fusion.1.sel_ref, bf16[456,384]{1,0:T(8,128)(2,1)} %bitcast.6, bf16[24,2304]{1,0:T(8,128)(2,1)} %w1_ref.1, f32[1,2304]{1,0:T(1,128)} %broadcast_in_dim.32.g1_ref, f32[1,2304]{1,0:T(1,128)} %broadcast_in_dim.33.s1_ref, f32[25,2304]{1,0:T(8,128)} %convert_element_type.9.dw_ref, ...), custom_call_target="tpu_custom_call" | custom-call | tf_op jit(solution)/shard_map/pallas_call | solution.py:352
  82.7 1.7 %slice_bitcast_fusion = bf16[1,19,19,384]{3,2,1,0:T(8,128)(2,1)} fusion(bf16[19,24,384]{2,1,0:T(8,128)(2,1)} %bitcast.7), kind=kLoop, calls=%fused_computation | loop fusion | bytes 554496 | tf_op jit(solution)/shard_map/broadcast_in_dim | solution.py:386
Async XLA Ops:
  0.0 8.4 %copy-start.2 = (f32[2304]{0:T(1024)S(1)}, f32[2304]{0:T(1024)}, u32[]{:S(2)}) copy-start(f32[2304]{0:T(1024)} %param.17) | copy-start | bytes 27652
  0.0 15.9 %copy-start.1 = (bf16[1,19,19,384]{3,2,1,0:T(8,128)(2,1)S(1)}, bf16[1,19,19,384]{3,2,1,0:T(8,128)(2,1)}, u32[]{:S(2)}) copy-start(bf16[1,19,19,384]{3,2,1,0:T(8,128)(2,1)} %param.15) | copy-start | bytes 831748
  15.9 1.1 %copy-start = (bf16[2304,96]{0,1:T(8,128)(2,1)S(1)}, bf16[2304,96]{0,1:T(8,128)(2,1)}, u32[]{:S(2)}) copy-start(bf16[2304,96]{0,1:T(8,128)(2,1)} %param.22) | copy-start | bytes 1327108

commit v2 on v1

--- a/solution.py
+++ b/solution.py
@@ -69,6 +69,8 @@
             slot = index(a + outer - d, 1 - b, c)
             await_slot(slot)
             send(slot, partner)
+
+    def fourth():
         for i in range(outer):
             for j in range(2):
                 await_slot(index(i, j, 1 - c))
@@ -77,15 +79,14 @@
         for move in sends:
             move.wait_send()
 
-    return first, second, third, finish
+    return first, second, third, fourth, finish
 
 
 def kernel(
     n, inside, height, breadth, pitch, groups,
-    sel_ref, x_ref, w1_ref, g1_ref, s1_ref, dw_ref, g2_ref, s2_ref,
-    sqw_ref, sqb_ref, exw_ref, exb_ref, w2_ref, g3_ref, s3_ref,
+    table_ref, x_ref, w1_ref, dw_ref, g1_ref, s1_ref, g2_ref, s2_ref, exb_ref, g3_ref, s3_ref, sqw_ref, sqb_ref, exw_ref, w2_ref,
     out_ref,
-    xp, w1, w2, expanded, filtered, wide, narrow, coef, pooled, proj,
+    vec_ref, xp, w1, w2, taps, expanded, filtered, wide, narrow, coef, pooled, proj,
     stats, last, w1_send, w1_recv, w2_send, w2_recv, st_send, st_recv,
 ):
     me = lax.axis_index("bn")
@@ -95,9 +96,9 @@
     width = exp // groups
     pixels = float(height * breadth)
 
-    def mask_of(lanes):
-        column = lax.broadcasted_iota(jnp.int32, (height, pitch, lanes), 1)
-        return (column < breadth).reshape(rows, lanes)
+    mine = table_ref[me]
+    member = [jnp.where(table_ref[k] == mine, 1.0, 0.0) for k in range(n)]
+    members = sum(member[1:], member[0])
 
     def masked(v):
         lanes = v.shape[1]
@@ -152,12 +153,14 @@
     def combine(buf, gain, shift):
         centre = jnp.zeros(gain.shape, jnp.float32)
         for k in range(n):
-            centre = centre + sel_ref[k] * buf[k, 0:1, :]
+            centre = centre + member[k] * buf[k, 0:1, :]
+        share = 1.0 / jnp.full(gain.shape, members, jnp.float32)
+        centre = centre * share
         spread = jnp.zeros(gain.shape, jnp.float32)
         for k in range(n):
             d = buf[k, 0:1, :] - centre
-            spread = spread + sel_ref[k] * (buf[k, 1:2, :] + d * d)
-        scale = lax.rsqrt(spread + epsilon) * gain
+            spread = spread + member[k] * (buf[k, 1:2, :] + d * d)
+        scale = lax.rsqrt(spread * share + epsilon) * gain
         return scale, shift - centre * scale
 
     r1, r2 = w1_ref.shape[0], w2_ref.shape[0]
@@ -192,9 +195,14 @@
             x_ref[...], spreader, preferred_element_type=jnp.float32
         ).astype(jnp.bfloat16)
     wide[...] = jnp.zeros_like(wide)
+    taps[...] = dw_ref[...].astype(jnp.float32)
+    for k, ref in enumerate((g1_ref, s1_ref, g2_ref, s2_ref, exb_ref, g3_ref, s3_ref)):
+        size = ref.shape[0]
+        vec_ref[k : k + 1, 0:size] = ref[...].reshape(1, size)
     if inside:
         g1[1]()
         g1[2]()
+        g1[3]()
 
     step = 256
     steps = width // step
@@ -226,7 +234,7 @@
     for g in range(groups):
         first_ex[g][1]()
         base = pl.ds(g * width, width)
-        scale, offset = combine(stats.at[0, g], g1_ref[:, base], s1_ref[:, base])
+        scale, offset = combine(stats.at[0, g], vec_ref[0:1, base], vec_ref[1:2, base])
         coef[0:1, base] = scale
         coef[1:2, base] = offset
 
@@ -247,7 +255,7 @@
                     part = None
                     for r in range(KERNEL):
                         tap = r * KERNEL + s
-                        term = window[r] * dw_ref[tap : tap + 1, cols]
+                        term = window[r] * taps[tap : tap + 1, cols]
                         part = term if part is None else part + term
                     turn = (MARGIN - s) % pitch
                     if turn:
@@ -262,13 +270,15 @@
             stats[1, g, me, :, inner] = moments(f.astype(jnp.float32))
 
         second_ex[g][0]()
-        if inside and g == groups - 1:
+        if inside and g == groups // 2:
             g2[1]()
 
     for g in range(groups):
         second_ex[g][1]()
         base = pl.ds(g * width, width)
-        scale, offset = combine(stats.at[1, g], g2_ref[:, base], s2_ref[:, base])
+        if inside and g == 0:
+            g2[2]()
+        scale, offset = combine(stats.at[1, g], vec_ref[2:3, base], vec_ref[3:4, base])
         coef[0:1, base] = scale
         coef[1:2, base] = offset
 
@@ -283,13 +293,16 @@
             )
 
     squeezed = silu(
-        jnp.dot(
-            pooled[...].astype(jnp.bfloat16), sqw_ref[...], preferred_element_type=jnp.float32
+        lax.dot_general(
+            pooled[...].astype(jnp.bfloat16),
+            sqw_ref[...],
+            (((1,), (1,)), ((), ())),
+            preferred_element_type=jnp.float32,
         )
         + sqb_ref[...]
     ).astype(jnp.bfloat16)
     gate = (
-        jnp.dot(squeezed, exw_ref[...], preferred_element_type=jnp.float32) + exb_ref[...]
+        jnp.dot(squeezed, exw_ref[...], preferred_element_type=jnp.float32) + vec_ref[4:5, :]
     )
     pooled[...] = 0.5 + 0.5 * jnp.tanh(0.5 * gate)
 
@@ -301,7 +314,7 @@
         ).astype(jnp.bfloat16)
 
     if inside:
-        g2[2]()
+        g2[3]()
         weights = w2[...].reshape(n * r2, channels)
     else:
         weights = w2_ref[...]
@@ -309,7 +322,7 @@
     last[me] = moments(proj[...])
     third_ex[0]()
     third_ex[1]()
-    scale, offset = combine(last, g3_ref[...], s3_ref[...])
+    scale, offset = combine(last, vec_ref[5:6, 0:channels], vec_ref[6:7, 0:channels])
     out_ref[...] = (
         x_ref[...].astype(jnp.float32) + (proj[...] * scale + offset)
     ).astype(jnp.bfloat16)
@@ -317,8 +330,8 @@
     for e in first_ex + second_ex + [third_ex]:
         e[2]()
     if inside:
-        g1[3]()
-        g2[3]()
+        g1[4]()
+        g2[4]()
 
 
 def on_device(
@@ -339,11 +352,6 @@
     if not inside:
         expand_weight = lax.all_gather(expand_weight, "bn", axis=0, tiled=True)
         project_weight = lax.all_gather(project_weight, "bn", axis=0, tiled=True)
-    me = lax.axis_index("bn")
-    ranks = jnp.arange(n, dtype=jnp.int32)
-    mine = jnp.sum(jnp.where(ranks == me, group_table, 0))
-    member = (group_table == mine).astype(jnp.float32)
-    sel = member / jnp.sum(member)
     x = jnp.pad(images[0], ((0, 0), (0, pitch - breadth), (0, 0))).reshape(rows, channels)
     f32, bf16 = jnp.float32, jnp.bfloat16
     small = (1, 16, LANES)
@@ -355,9 +363,11 @@
         in_specs=[pl.BlockSpec(memory_space=pltpu.SMEM)] + [vmem] * 14,
         out_specs=vmem,
         scratch_shapes=[
+            pltpu.VMEM((8, exp), f32),
             pltpu.VMEM((rows, n * slab) if inside else (16, LANES), bf16),
             pltpu.VMEM((n, slab, exp) if inside else small, bf16),
             pltpu.VMEM((n, r2, channels) if inside else small, bf16),
+            pltpu.VMEM(depth_weight.shape, f32),
             pltpu.VMEM((rows, exp), bf16),
             pltpu.VMEM((rows, exp), bf16),
             pltpu.VMEM((rows + 2 * MARGIN * pitch, LANES), f32),
@@ -378,10 +388,10 @@
             collective_id=0, has_side_effects=True, vmem_limit_bytes=60 * 1024 * 1024
         ),
     )(
-        sel, x, expand_weight, expand_gain[None], expand_shift[None],
-        depth_weight.astype(f32), depth_gain[None], depth_shift[None],
-        squeeze_weight, squeeze_bias[None], excite_weight, excite_bias[None],
-        project_weight, project_gain[None], project_shift[None],
+        group_table, x, expand_weight, depth_weight,
+        expand_gain, expand_shift, depth_gain, depth_shift, excite_bias,
+        project_gain, project_shift,
+        squeeze_weight.T, squeeze_bias[None], excite_weight, project_weight,
     )
     return out.reshape(height, pitch, channels)[None, :, :breadth]
 

time: 85 us -> 68.8 us (0.81)
  local copies, waits for them, and re-layouts: 12.3 us -> 3.5 us
  other arithmetic: 6.79 us -> 0 us
    broadcast_in_dim x7 -> x0, local copies, waits for them, and re-layouts: 8.33 us -> none  [the longest x1 1.31 us: on_device(): excite_bias[None]]
    reduce_sum x2 -> x0, other arithmetic: 3.33 us -> none  [the longest x1 1.98 us: on_device(): sel = member / jnp.sum(member)]
    div x1 -> x0, other arithmetic: 1.82 us -> none  [on_device(): sel = member / jnp.sum(member)]
    convert_element_type x1 -> x0, other arithmetic: 1.64 us -> none  [on_device(): depth_weight.astype(f32)]
    unnamed x7 -> x0, local copies, waits for them, and re-layouts: 1.43 us -> none
    pad x1, local copies, waits for them, and re-layouts: 0.77 us -> 1.75 us  [on_device(): jnp.pad(images[0], ((0, 0), (0, pitch - breadth), (0, 0)))]
where the time goes in v2:
time: 68.8 us; the launch traced here: 68.6 us
  Pallas kernels  65.1 us (95%)
  local copies, waits for them, and re-layouts  3.5 us (5%)
    pallas_call x1, Pallas kernels, on_device(): pl.pallas_call(functools.partial(kernel, n, inside, height, breadth, pitc...  65.1 us
    pad x1, local copies, waits for them, and re-layouts, on_device(): jnp.pad(images[0], ((0, 0), (0, pitch - breadth), (0, 0)))  1.75 us
    broadcast_in_dim x1, local copies, waits for them, and re-layouts, on_device(): return out.reshape(height, pitch, channels)[None, :, :breadth]  1.75 us

profile of v2, /device:TPU:0, one launch (start us, length us, event | category | flops | bytes accessed | tf_op | source)
XLA Modules:
  0.0 68.6 jit_solution(1257856562799768965)
XLA Ops:
  0.0 1.7 %pad.4 = bf16[19,24,384]{2,1,0:T(8,128)(2,1)} pad(bf16[19,19,384]{2,1,0:T(8,128)(2,1)} %bitcast.10, bf16[]{:T(256)} %constant.2.clone.1), padding=0_0x0_5x0_0 | pad | bytes 627458 | tf_op jit(solution)/shard_map/jit(_pad)/pad | solution.py:355
  1.7 65.1 %shard_map.145 = bf16[456,384]{1,0:T(8,128)(2,1)} custom-call(s32[16]{0:T(128)} %table_ref.1, bf16[456,384]{1,0:T(8,128)(2,1)} %bitcast.7, bf16[24,2304]{1,0:T(8,128)(2,1)} %w1_ref.1, bf16[25,2304]{1,0:T(8,128)(2,1)} %dw_ref.1, f32[2304]{0:T(1024)} %g1_ref.1, f32[2304]{0:T(1024)} %s1_ref.1, f32[2304]{0:T(1024)} %g2_ref.1, f32[2304]{0:T(1024)} %s2_ref.1, ...), custom_call_target="tpu_custom_call" | custom-call | tf_op jit(solution)/shard_map/pallas_call | solution.py:360
  66.8 1.7 %slice_bitcast_fusion = bf16[1,19,19,384]{3,2,1,0:T(8,128)(2,1)} fusion(bf16[19,24,384]{2,1,0:T(8,128)(2,1)} %bitcast.8), kind=kLoop, calls=%fused_computation | loop fusion | bytes 554496 | tf_op jit(solution)/shard_map/broadcast_in_dim | solution.py:396
